TPU v7x, 128 devices: a whole 4x4x4 slice. The times are simulated.
128 devices in a mesh: kx: 8 (over z_lo, y), ky: 16 (over x, z_hi, core).
Axes of the slice: x: 4, y: 4, z: 4 (z_hi: 2, z_lo: 2; z = z_hi * 2 + z_lo), core: 2. Of those that a mesh axis runs over, the one named last changes fastest.
Arguments:
- wannier: bfloat16 [32, 128, 64, 128], P('kx', 'ky'), may hold values from -0.5 to 0.5
- coupling: bfloat16 [3, 32, 128, 6, 64, 128], P(None, 'kx', 'ky'), may hold values from -6 to 6
- kq_map: int32 [3, 4096], replicated, may hold values from 0 to 4095, as said below
Outputs:
- rotated: bfloat16 [3, 32, 128, 6, 64, 128], P(None, 'kx', 'ky')
Inputs may be any that keep to these rules, and one draw needn't show every extreme that they name: For every q there are offsets a and b with kq_map[q, x * 128 + y] = ((x + a) mod 32) * 128 + (y + b) mod 128.
All inputs are finite; a program needn't handle non-finite values.
Results may differ from a plain program's by a relative error of at most 0.0049.
Values may be sent and summed in bfloat16 or wider, within the bound.
No kernel may reach another device: no remote copies, remote signals or barrier semaphores. Data moves between devices by JAX's collectives and lax.ppermute only.
A program may use at most 192 MiB of HBM per device.

v0:
```python
import jax
import jax.numpy as jnp
from jax import lax
from jax.sharding import PartitionSpec as P


def right_factor(matrix):
    half_width = matrix.shape[-1] // 2
    lower_half = jnp.concatenate([-matrix[..., half_width:], matrix[..., :half_width]], axis=-1)
    return jnp.concatenate([matrix, lower_half], axis=-2)


def rotate(block_g, factor, partner):
    half_width = partner.shape[-1] // 2
    half_turn = jnp.einsum(
        "xymac,xycd->xymad", block_g, factor, preferred_element_type=jnp.float32
    ).astype(jnp.bfloat16)
    stacked = jnp.concatenate(
        [
            half_turn,
            jnp.concatenate([half_turn[..., half_width:], -half_turn[..., :half_width]], axis=-1),
        ],
        axis=-2,
    )
    partner_rows = jnp.concatenate([partner[..., :half_width], partner[..., half_width:]], axis=-2)
    return jnp.einsum(
        "xyca,xymcd->xymad", partner_rows, stacked, preferred_element_type=jnp.float32
    ).astype(jnp.bfloat16)


def per_device(wannier, coupling, kq_map):
    rows_x = wannier.shape[0]
    cols_y = wannier.shape[1]
    count_x = lax.axis_size("kx")
    count_y = lax.axis_size("ky")
    total_x = rows_x * count_x
    total_y = cols_y * count_y
    index_x = lax.axis_index("kx")
    index_y = lax.axis_index("ky")
    factor = right_factor(wannier)
    results = []
    for qpoint in range(coupling.shape[0]):
        offset = kq_map[qpoint, 0]
        offset_x = offset // total_y
        offset_y = offset % total_y
        segment = lax.all_gather(wannier, "kx", axis=0, tiled=True)
        wanted = (index_x * rows_x + jnp.arange(rows_x, dtype=jnp.int32) + offset_x) % total_x
        held_rows = jnp.arange(segment.shape[0], dtype=jnp.int32)
        chooser = (wanted[:, None] == held_rows[None, :]).astype(jnp.bfloat16)
        row_aligned = jnp.einsum(
            "rj,jyab->ryab", chooser, segment, preferred_element_type=jnp.float32
        ).astype(jnp.bfloat16)
        pick_segment = lax.all_gather(row_aligned, "ky", axis=1, tiled=True)
        pick_wanted = (index_y * cols_y + jnp.arange(cols_y, dtype=jnp.int32) + offset_y) % total_y
        held_cols = jnp.arange(pick_segment.shape[1], dtype=jnp.int32)
        pick_chooser = (pick_wanted[:, None] == held_cols[None, :]).astype(jnp.bfloat16)
        partner = jnp.einsum(
            "rj,xjab->xrab", pick_chooser, pick_segment, preferred_element_type=jnp.float32
        ).astype(jnp.bfloat16)
        results.append(rotate(coupling[qpoint], factor, partner))
    return jnp.stack(results, axis=0)


def solution(mesh):
    in_specs = (P("kx", "ky", None, None), P(None, "kx", "ky", None, None, None), P())
    out_specs = P(None, "kx", "ky", None, None, None)
    return jax.shard_map(
        per_device, mesh=mesh, in_specs=in_specs, out_specs=out_specs, check_vma=False
    )
```

profile of v0, /device:TPU:1, one launch (start us, length us, event | category | flops | bytes accessed | tf_op | source)
XLA Modules:
  0.0 344.5 jit_solution(5136347526506224214)
XLA Ops:
  7.3 1.3 fusion.84
  13.7 50.9 %all-gather.5.cloned.1.call-done = bf16[32,8,64,128]{3,2,1,0:T(8,128)(2,1)} async-done(((bf16[4,8,64,128]{3,2,1,0:T(8,128)(2,1)}), bf16[32,8,64,128]{3,2,1,0:T(8,128)(2,1)}) %all-gather.5.cloned.1.call-update) | async-done | bytes 4194320 | tf_op jit(solution)/shard_map/all_gather | solution.py:46
  64.7 4.6 %fusion.20 = bf16[4,8,64,128]{3,0,2,1:T(4,128)(2,1)S(1)} fusion(bf16[32,8,64,128]{3,2,1,0:T(8,128)(2,1)} %all-gather.5.cloned.1.call-done, s32[4]{0:T(128)S(1)} %get-tuple-element.23), kind=kOutput, calls=%fused_computation.21 | convolution fusion | flops 16777344 | bytes 4718608 | tf_op jit(solution)/shard_map/rj,jyab->ryab/dot_general | solution.py:50
  69.3 1.2 copy.46
  73.1 4.6 %fusion.22 = bf16[4,8,64,128]{3,0,2,1:T(4,128)(2,1)S(1)} fusion(bf16[32,8,64,128]{3,2,1,0:T(8,128)(2,1)} %all-gather.5.cloned.1.call-done, s32[4]{0:T(128)S(1)} %and_select_fusion.5), kind=kOutput, calls=%fused_computation.23 | convolution fusion | flops 16777344 | bytes 4718608 | tf_op jit(solution)/shard_map/rj,jyab->ryab/dot_general | solution.py:50
  79.2 4.8 %fusion.18 = bf16[4,8,64,128]{3,0,2,1:T(4,128)(2,1)S(1)} fusion(bf16[32,8,64,128]{3,2,1,0:T(8,128)(2,1)} %all-gather.5.cloned.1.call-done, s32[4]{0:T(128)S(1)} %get-tuple-element.22), kind=kOutput, calls=%fused_computation.19 | convolution fusion | flops 16777344 | bytes 4718608 | tf_op jit(solution)/shard_map/rj,jyab->ryab/dot_general | solution.py:50
  85.5 3.2 convert_bitcast_fusion.3
  88.7 2.9 convert_bitcast_fusion.1
  91.7 4.1 %convert_bitcast_fusion.5 = bf16[4,8,6,64,128]{4,3,2,1,0:T(8,128)(2,1)S(1)} fusion(bf16[3,4,8,6,64,128]{5,4,3,2,1,0:T(8,128)(2,1)} %param.4, bf16[4,8,64,64]{3,2,1,0:T(8,128)(2,1)S(1)} %get-tuple-element.18, bf16[4,8,64,64]{3,2,1,0:T(8,128)(2,1)S(1)} %get-tuple-element.17, bf16[4,8,64,128]{3,2,1,0:T(8,128)(2,1)S(1)} %copy-done.5), kind=kOutput, calls=%fused_computation.41 | convolution fusion | flops 407371776 | bytes 7340032 | tf_op jit(solution)/shard_map/xymac,xycd->xymad/dot_general | solution.py:15
  95.8 3.8 %fusion.78 = (bf16[4,8,6,64,64]{4,3,2,1,0:T(8,128)(2,1)}, bf16[4,8,6,64,64]{4,3,2,1,0:T(8,128)(2,1)}) fusion(bf16[4,8,6,64,128]{4,3,2,1,0:T(8,128)(2,1)S(1)} %convert_bitcast_fusion.5), kind=kLoop, calls=%fused_computation.107 | loop fusion | flops 786432 | bytes 6291456 | tf_op jit(solution)/shard_map/slice | solution.py:21
  99.6 3.8 %fusion.80 = (bf16[4,8,6,64,64]{4,3,2,1,0:T(8,128)(2,1)}, bf16[4,8,6,64,64]{4,3,2,1,0:T(8,128)(2,1)}) fusion(bf16[4,8,6,64,128]{4,3,2,1,0:T(8,128)(2,1)S(1)} %convert_bitcast_fusion.1), kind=kLoop, calls=%fused_computation.109 | loop fusion | flops 786432 | bytes 6291456 | tf_op jit(solution)/shard_map/slice | solution.py:21
  103.4 3.8 %fusion.79 = (bf16[4,8,6,64,64]{4,3,2,1,0:T(8,128)(2,1)}, bf16[4,8,6,64,64]{4,3,2,1,0:T(8,128)(2,1)}) fusion(bf16[4,8,6,64,128]{4,3,2,1,0:T(8,128)(2,1)S(1)} %convert_bitcast_fusion.3), kind=kLoop, calls=%fused_computation.108 | loop fusion | flops 786432 | bytes 6291456 | tf_op jit(solution)/shard_map/slice | solution.py:21
  107.2 41.8 %all-gather.9.cloned.1.call-done = bf16[4,128,64,128]{3,1,2,0:T(8,128)(2,1)} async-done(((bf16[4,8,64,128]{3,1,2,0:T(8,128)(2,1)}), bf16[4,128,64,128]{3,1,2,0:T(8,128)(2,1)}) %all-gather.9.cloned.1.call-update) | async-done | bytes 8388624 | tf_op jit(solution)/shard_map/all_gather | solution.py:53
  149.1 4.6 %fusion.46 = bf16[4,8,64,128]{3,1,2,0:T(8,128)(2,1)S(1)} fusion(bf16[4,128,64,128]{3,1,2,0:T(8,128)(2,1)} %all-gather.9.cloned.1.call-done, s32[8]{0:T(128)S(1)} %and_select_fusion.2), kind=kOutput, calls=%fused_computation.47 | convolution fusion | flops 67372032 | bytes 8912928 | tf_op jit(solution)/shard_map/rj,xjab->xrab/dot_general | solution.py:57
  153.7 1.2 fusion.82
  154.9 73.9 %all-gather.7.cloned.1.call-done = bf16[4,128,64,128]{3,1,2,0:T(8,128)(2,1)} async-done(((bf16[4,8,64,128]{3,1,2,0:T(8,128)(2,1)}), bf16[4,128,64,128]{3,1,2,0:T(8,128)(2,1)}) %all-gather.7.cloned.1.call-update) | async-done | bytes 8388624 | tf_op jit(solution)/shard_map/all_gather | solution.py:53
  228.8 4.8 %fusion.45 = bf16[4,8,64,128]{3,1,2,0:T(8,128)(2,1)S(1)} fusion(bf16[4,128,64,128]{3,1,2,0:T(8,128)(2,1)} %all-gather.7.cloned.1.call-done, s32[8]{0:T(128)S(1)} %and_select_fusion.4), kind=kOutput, calls=%fused_computation.46 | convolution fusion | flops 67372032 | bytes 8912928 | tf_op jit(solution)/shard_map/rj,xjab->xrab/dot_general | solution.py:57
  233.6 1.2 fusion.81
  234.8 73.6 %all-gather.11.cloned.1.call-done = bf16[4,128,64,128]{3,1,2,0:T(8,128)(2,1)} async-done(((bf16[4,8,64,128]{3,1,2,0:T(8,128)(2,1)}), bf16[4,128,64,128]{3,1,2,0:T(8,128)(2,1)}) %all-gather.11.cloned.1.call-update) | async-done | bytes 8388624 | tf_op jit(solution)/shard_map/all_gather | solution.py:53
  308.4 4.8 %fusion.47 = bf16[4,8,64,128]{3,1,2,0:T(8,128)(2,1)S(1)} fusion(bf16[4,128,64,128]{3,1,2,0:T(8,128)(2,1)} %all-gather.11.cloned.1.call-done, s32[8]{0:T(128)S(1)} %and_select_fusion), kind=kOutput, calls=%fused_computation.48 | convolution fusion | flops 67372032 | bytes 8912928 | tf_op jit(solution)/shard_map/rj,xjab->xrab/dot_general | solution.py:57
  316.1 4.4 %convert_bitcast_fusion.4 = bf16[1,4,8,6,64,128]{5,4,3,2,1,0:T(8,128)(2,1)} fusion(bf16[4,8,6,64,64]{4,3,2,1,0:T(8,128)(2,1)S(1)} %copy-done.11, bf16[4,8,6,64,64]{4,3,2,1,0:T(8,128)(2,1)S(1)} %copy-done.10, bf16[4,8,6,64,128]{4,3,2,1,0:T(8,128)(2,1)S(1)} %copy-done.3, bf16[4,8,128,64,1]{3,1,2,0,4:T(8,128)(2,1)S(1)} %maximum_bitcast_fusion), kind=kOutput, calls=%fused_computation.40 | convolution fusion | flops 423100416 | bytes 9961472 | tf_op jit(solution)/shard_map/xyca,xymcd->xymad/dot_general | solution.py:26
  320.5 4.5 %convert_bitcast_fusion = bf16[1,4,8,6,64,128]{5,4,3,2,1,0:T(8,128)(2,1)} fusion(bf16[4,8,6,64,64]{4,3,2,1,0:T(8,128)(2,1)S(1)} %copy-done.9, bf16[4,8,6,64,64]{4,3,2,1,0:T(8,128)(2,1)S(1)} %copy-done.8, bf16[4,8,6,64,128]{4,3,2,1,0:T(8,128)(2,1)S(1)} %copy-done.1, bf16[4,8,128,64,1]{3,1,2,0,4:T(8,128)(2,1)S(1)} %maximum_bitcast_fusion.3), kind=kOutput, calls=%fused_computation.34 | convolution fusion | flops 423100416 | bytes 9961472 | tf_op jit(solution)/shard_map/xyca,xymcd->xymad/dot_general | solution.py:26
  325.0 4.5 %convert_bitcast_fusion.2 = bf16[1,4,8,6,64,128]{5,4,3,2,1,0:T(8,128)(2,1)} fusion(bf16[4,8,6,64,64]{4,3,2,1,0:T(8,128)(2,1)S(1)} %copy-done.7, bf16[4,8,6,64,64]{4,3,2,1,0:T(8,128)(2,1)S(1)} %copy-done.6, bf16[4,8,6,64,128]{4,3,2,1,0:T(8,128)(2,1)S(1)} %convert_bitcast_fusion.3, bf16[4,8,128,64,1]{3,1,2,0,4:T(8,128)(2,1)S(1)} %maximum_bitcast_fusion.2), kind=kOutput, calls=%fused_computation.37 | convolution fusion | flops 423100416 | bytes 9961472 | tf_op jit(solution)/shard_map/xyca,xymcd->xymad/dot_general | solution.py:26
  329.4 8.5 %pad_maximum_fusion = bf16[3,4,8,6,64,128]{5,4,3,2,1,0:T(8,128)(2,1)} fusion(bf16[1,4,8,6,64,128]{5,4,3,2,1,0:T(8,128)(2,1)} %convert_bitcast_fusion, bf16[1,4,8,6,64,128]{5,4,3,2,1,0:T(8,128)(2,1)} %convert_bitcast_fusion.2, bf16[1,4,8,6,64,128]{5,4,3,2,1,0:T(8,128)(2,1)} %convert_bitcast_fusion.4), kind=kLoop, calls=%fused_computation | loop fusion | flops 9437184 | bytes 18874368 | tf_op jit(solution)/shard_map/stack | solution.py:61
  (52 shorter events, 6.5 us)
Async XLA Ops:
  6.5 58.1 %all-gather.5.cloned.1.call-start = ((), (), s32[]{:S(2)}) async-start(), calls=%async_computation | async-start | bytes 4718592 | tf_op jit(solution)/shard_map/all_gather | solution.py:46
  7.3 141.8 %all-gather.9.cloned.1.call-start = ((), (), s32[]{:S(2)}) async-start(), calls=%async_computation.2 | async-start | bytes 8912896 | tf_op jit(solution)/shard_map/all_gather | solution.py:53
  70.5 158.3 %all-gather.7.cloned.1.call-start = ((), (), s32[]{:S(2)}) async-start(), calls=%async_computation.1 | async-start | bytes 8912896 | tf_op jit(solution)/shard_map/all_gather | solution.py:53
  77.8 7.5 %copy-start.4 = (bf16[4,8,64,128]{3,2,1,0:T(8,128)(2,1)S(1)}, bf16[4,8,64,128]{3,2,1,0:T(8,128)(2,1)}, u32[]{:S(2)}) copy-start(bf16[4,8,64,128]{3,2,1,0:T(8,128)(2,1)} %param.3) | copy-start | bytes 1572868
  79.0 229.5 %all-gather.11.cloned.1.call-start = ((), (), s32[]{:S(2)}) async-start(), calls=%async_computation.3 | async-start | bytes 8912896 | tf_op jit(solution)/shard_map/all_gather | solution.py:53
  85.5 3.2 copy-start.5
  91.7 7.9 %copy-start = (bf16[4,8,6,64,128]{4,3,2,1,0:T(8,128)(2,1)}, bf16[4,8,6,64,128]{4,3,2,1,0:T(8,128)(2,1)S(1)}, u32[]{:S(2)}) copy-start(bf16[4,8,6,64,128]{4,3,2,1,0:T(8,128)(2,1)S(1)} %convert_bitcast_fusion.1) | copy-start | bytes 9437188
  95.7 3.9 %copy-start.2 = (bf16[4,8,6,64,128]{4,3,2,1,0:T(8,128)(2,1)}, bf16[4,8,6,64,128]{4,3,2,1,0:T(8,128)(2,1)S(1)}, u32[]{:S(2)}) copy-start(bf16[4,8,6,64,128]{4,3,2,1,0:T(8,128)(2,1)S(1)} %convert_bitcast_fusion.5) | copy-start | bytes 9437188
  308.4 5.0 %copy-start.12 = (bf16[4,8,64,64]{3,1,2,0:T(8,128)(2,1)S(1)}, bf16[4,8,64,64]{3,1,2,0:T(8,128)(2,1)}, u32[]{:S(2)}) copy-start(bf16[4,8,64,64]{3,1,2,0:T(8,128)(2,1)} %get-tuple-element.13) | copy-start | bytes 786436
  308.4 5.0 %copy-start.13 = (bf16[4,8,64,64]{3,1,2,0:T(8,128)(2,1)S(1)}, bf16[4,8,64,64]{3,1,2,0:T(8,128)(2,1)}, u32[]{:S(2)}) copy-start(bf16[4,8,64,64]{3,1,2,0:T(8,128)(2,1)} %get-tuple-element.14) | copy-start | bytes 786436
  308.4 5.2 %copy-start.14 = (bf16[4,8,64,64]{3,1,2,0:T(8,128)(2,1)S(1)}, bf16[4,8,64,64]{3,1,2,0:T(8,128)(2,1)}, u32[]{:S(2)}) copy-start(bf16[4,8,64,64]{3,1,2,0:T(8,128)(2,1)} %get-tuple-element.11) | copy-start | bytes 786436
  308.4 5.3 %copy-start.15 = (bf16[4,8,64,64]{3,1,2,0:T(8,128)(2,1)S(1)}, bf16[4,8,64,64]{3,1,2,0:T(8,128)(2,1)}, u32[]{:S(2)}) copy-start(bf16[4,8,64,64]{3,1,2,0:T(8,128)(2,1)} %get-tuple-element.12) | copy-start | bytes 786436
  308.4 5.7 %copy-start.11 = (bf16[4,8,6,64,64]{4,3,2,1,0:T(8,128)(2,1)S(1)}, bf16[4,8,6,64,64]{4,3,2,1,0:T(8,128)(2,1)}, u32[]{:S(2)}) copy-start(bf16[4,8,6,64,64]{4,3,2,1,0:T(8,128)(2,1)} %get-tuple-element.6) | copy-start | bytes 4718596
  313.2 1.9 copy-start.3
  313.2 2.8 copy-start.10
  316.1 4.4 %copy-start.1 = (bf16[4,8,6,64,128]{4,3,2,1,0:T(8,128)(2,1)S(1)}, bf16[4,8,6,64,128]{4,3,2,1,0:T(8,128)(2,1)}, u32[]{:S(2)}) copy-start(bf16[4,8,6,64,128]{4,3,2,1,0:T(8,128)(2,1)} %copy-done) | copy-start | bytes 9437188
  316.1 4.4 %copy-start.8 = (bf16[4,8,6,64,64]{4,3,2,1,0:T(8,128)(2,1)S(1)}, bf16[4,8,6,64,64]{4,3,2,1,0:T(8,128)(2,1)}, u32[]{:S(2)}) copy-start(bf16[4,8,6,64,64]{4,3,2,1,0:T(8,128)(2,1)} %get-tuple-element.9) | copy-start | bytes 4718596
  316.1 4.5 %copy-start.9 = (bf16[4,8,6,64,64]{4,3,2,1,0:T(8,128)(2,1)S(1)}, bf16[4,8,6,64,64]{4,3,2,1,0:T(8,128)(2,1)}, u32[]{:S(2)}) copy-start(bf16[4,8,6,64,64]{4,3,2,1,0:T(8,128)(2,1)} %get-tuple-element.10) | copy-start | bytes 4718596
  320.5 4.5 %copy-start.6 = (bf16[4,8,6,64,64]{4,3,2,1,0:T(8,128)(2,1)S(1)}, bf16[4,8,6,64,64]{4,3,2,1,0:T(8,128)(2,1)}, u32[]{:S(2)}) copy-start(bf16[4,8,6,64,64]{4,3,2,1,0:T(8,128)(2,1)} %get-tuple-element.7) | copy-start | bytes 4718596
  320.5 4.5 %copy-start.7 = (bf16[4,8,6,64,64]{4,3,2,1,0:T(8,128)(2,1)S(1)}, bf16[4,8,6,64,64]{4,3,2,1,0:T(8,128)(2,1)}, u32[]{:S(2)}) copy-start(bf16[4,8,6,64,64]{4,3,2,1,0:T(8,128)(2,1)} %get-tuple-element.8) | copy-start | bytes 4718596
Sparse Core Ops, SparseCore 0:
  9.0 55.6 all-gather.4
  70.6 78.4 all-gather.8
  151.3 77.4 all-gather.6
  230.9 77.4 all-gather.10
where the time goes:
time: 345 us; the launch traced here: 344 us
  waiting for transfers between devices  241 us (70%)
  matrix products  51.8 us (15%)
  between operations  21 us (6%)
  other arithmetic  20.9 us (6%)
  local copies, waits for them, and re-layouts  9.41 us (3%)
    all_gather x3, waiting for transfers between devices, per_device(): pick_segment = lax.all_gather(row_aligned, 'ky', axis=1, tiled=True)  189 us
    all_gather x1, waiting for transfers between devices, per_device(): segment = lax.all_gather(wannier, 'kx', axis=0, tiled=True)  50.9 us
    dot_general x3, matrix products, per_device(): jnp.einsum('rj,xjab->xrab', pick_chooser, pick_segment, preferred_element...  14.2 us
    dot_general x3, matrix products, per_device(): jnp.einsum('rj,jyab->ryab', chooser, segment, preferred_element_type=jnp....  14.1 us
    dot_general x3, matrix products, rotate(): jnp.einsum('xyca,xymcd->xymad', partner_rows, stacked, preferred_element_...  13.3 us
    slice x3, other arithmetic, rotate(): half_turn[..., half_width:]  11.5 us
    dot_general x3, matrix products, rotate(): jnp.einsum('xymac,xycd->xymad', block_g, factor, preferred_element_type=j...  10.2 us
    another operation x1, other arithmetic, per_device(): return jnp.stack(results, axis=0)  8.51 us
  transfers between devices with their start and end apart: 4, of which 4 were waited for; matrix products, arithmetic and copies ran while one was open for 14% of the time, Pallas kernels for 0%

commit v1 on v0

v1 whole, which is shorter than its diff:
```python
import jax
import jax.numpy as jnp
from jax import lax
from jax.experimental import pallas as pl
from jax.experimental.pallas import tpu as pltpu
from jax.sharding import PartitionSpec as P

AXES = ("kx", "ky")
MIB = 1024 * 1024
H_GROUPS = 8
R_GROUPS = 16


def stream(in_ref, out_ref, in_buf, out_buf, in_sem, out_sem, work):
    groups = in_sem.shape[0]
    size = in_buf.shape[1] // groups

    def fetch(i):
        at = pl.ds(i * size, size)
        return pltpu.make_async_copy(in_ref.at[:, at], in_buf.at[:, at], in_sem.at[i])

    def send(i):
        at = pl.ds(i * size, size)
        return pltpu.make_async_copy(out_buf.at[:, at], out_ref.at[:, at], out_sem.at[i])

    def start(i, carry):
        fetch(i).start()
        return carry

    def step(i, carry):
        fetch(i).wait()
        for k in range(size):
            work(i * size + k)
        send(i).start()
        return carry

    def finish(i, carry):
        send(i).wait()
        return carry

    lax.fori_loop(0, groups, start, 0)
    lax.fori_loop(0, groups, step, 0)
    lax.fori_loop(0, groups, finish, 0)


def stream_scratch(shape_in, shape_out, groups):
    return [
        pltpu.VMEM(shape_in, jnp.bfloat16),
        pltpu.VMEM(shape_out, jnp.bfloat16),
        pltpu.SemaphoreType.DMA((groups,)),
        pltpu.SemaphoreType.DMA((groups,)),
    ]


def half_turn_kernel(u_ref, g_ref, o_ref, g_buf, o_buf, in_sem, out_sem):
    n_q, _, modes, nb, width = g_buf.shape

    def work(k):
        u = u_ref[k]
        turned = jnp.concatenate([-u[:, nb:], u[:, :nb]], axis=1)
        factor = jnp.concatenate([u, turned], axis=0)
        for q in range(n_q):
            rows = g_buf[q, k].reshape(modes * nb, width)
            half = jnp.dot(rows, factor, preferred_element_type=jnp.float32).astype(jnp.bfloat16)
            for p in range(modes // 2):
                one = half[2 * p * nb : (2 * p + 1) * nb]
                two = half[(2 * p + 1) * nb : (2 * p + 2) * nb]
                o_buf[q, k, p, :nb] = jnp.concatenate([one[:, :nb], two[:, :nb]], axis=1)
                o_buf[q, k, p, nb:] = jnp.concatenate([one[:, nb:], two[:, nb:]], axis=1)

    stream(g_ref, o_ref, g_buf, o_buf, in_sem, out_sem, work)


def half_turns(wannier, coupling):
    n_q, n_k, modes, nb, width = coupling.shape
    paired = (n_q, n_k, modes // 2, 2 * nb, width)
    return pl.pallas_call(
        half_turn_kernel,
        in_specs=[pl.BlockSpec(memory_space=pltpu.VMEM), pl.BlockSpec(memory_space=pltpu.HBM)],
        out_specs=pl.BlockSpec(memory_space=pltpu.HBM),
        out_shape=jax.ShapeDtypeStruct(paired, jnp.bfloat16),
        scratch_shapes=stream_scratch(coupling.shape, paired, H_GROUPS),
        compiler_params=pltpu.CompilerParams(vmem_limit_bytes=56 * MIB),
        cost_estimate=pl.CostEstimate(
            flops=4 * n_q * n_k * modes * nb * width * width,
            bytes_accessed=4 * n_q * n_k * modes * nb * width,
            transcendentals=0,
        ),
        name="half_turns",
    )(wannier, coupling)


def shuffle_kernel(shift_ref, held_ref, o_ref):
    n_x, n_y, rows, _ = held_ref.shape
    for q in range(o_ref.shape[2] // rows):
        shift_x = shift_ref[q, 0]
        shift_y = shift_ref[q, 1]
        for y in range(n_y):
            from_y = lax.rem(shift_y + y, n_y)
            for x in range(n_x):
                o_ref[x, y, q * rows : (q + 1) * rows] = held_ref[lax.rem(shift_x + x, n_x), from_y]


def shuffle(shifts, held, n_q):
    n_x, n_y, rows, width = held.shape
    return pl.pallas_call(
        shuffle_kernel,
        in_specs=[
            pl.BlockSpec(memory_space=pltpu.SMEM),
            pl.BlockSpec(memory_space=pltpu.VMEM),
        ],
        out_specs=pl.BlockSpec(memory_space=pltpu.VMEM),
        out_shape=jax.ShapeDtypeStruct((n_x, n_y, n_q * rows, width), held.dtype),
        compiler_params=pltpu.CompilerParams(vmem_limit_bytes=8 * MIB),
        name="shuffle",
    )(shifts, held)


def rotate_kernel(shift_ref, v_ref, h_ref, o_ref, h_buf, o_buf, in_sem, out_sem, *, n_x, n_y):
    n_q, _, modes, nb, width = o_buf.shape
    rows = v_ref.shape[2] // n_q

    def work(k):
        for q in range(n_q):
            at_x = lax.rem(k // n_y + shift_ref[q, 2], n_x)
            at_y = lax.rem(lax.rem(k, n_y) + shift_ref[q, 3], n_y)
            v = v_ref[at_x * n_y + at_y, :, q * rows : (q + 1) * rows].reshape(nb, width)
            left = jnp.concatenate(
                [
                    jnp.concatenate([v[:, :nb], -v[:, nb:]], axis=1),
                    jnp.concatenate([v[:, nb:], v[:, :nb]], axis=1),
                ],
                axis=0,
            )
            right = jnp.concatenate([h_buf[q, k, p] for p in range(modes // 2)], axis=1)
            out = lax.dot_general(
                left, right, (((0,), (0,)), ((), ())), preferred_element_type=jnp.float32
            ).astype(jnp.bfloat16)
            for p in range(modes // 2):
                real = out[:nb, p * width : (p + 1) * width]
                imag = out[nb:, p * width : (p + 1) * width]
                o_buf[q, k, 2 * p] = jnp.concatenate([real[:, :nb], imag[:, :nb]], axis=1)
                o_buf[q, k, 2 * p + 1] = jnp.concatenate([real[:, nb:], imag[:, nb:]], axis=1)

    stream(h_ref, o_ref, h_buf, o_buf, in_sem, out_sem, work)


def rotate(shifts, partner, halves, n_x, n_y):
    n_q, n_k, pairs, _, width = halves.shape
    modes, nb = 2 * pairs, width // 2
    shape = (n_q, n_k, modes, nb, width)
    return pl.pallas_call(
        lambda *refs: rotate_kernel(*refs, n_x=n_x, n_y=n_y),
        in_specs=[
            pl.BlockSpec(memory_space=pltpu.SMEM),
            pl.BlockSpec(memory_space=pltpu.VMEM),
            pl.BlockSpec(memory_space=pltpu.HBM),
        ],
        out_specs=pl.BlockSpec(memory_space=pltpu.HBM),
        out_shape=jax.ShapeDtypeStruct(shape, jnp.bfloat16),
        scratch_shapes=stream_scratch(halves.shape, shape, R_GROUPS),
        compiler_params=pltpu.CompilerParams(vmem_limit_bytes=50 * MIB),
        cost_estimate=pl.CostEstimate(
            flops=4 * n_q * n_k * modes * nb * width * nb,
            bytes_accessed=4 * n_q * n_k * modes * nb * width,
            transcendentals=0,
        ),
        name="rotate",
    )(shifts, partner, halves)


def per_device(wannier, coupling, kq_map):
    rows_x, cols_y, nb, width = wannier.shape
    n_q = coupling.shape[0]
    modes = coupling.shape[3]
    count_x = lax.axis_size("kx")
    count_y = lax.axis_size("ky")
    devices = count_x * count_y
    n_k = rows_x * cols_y
    pieces = devices // n_k
    rows = nb // pieces
    total_y = cols_y * count_y
    me = lax.axis_index("kx") * count_y + lax.axis_index("ky")
    point = me // pieces
    offset = kq_map[:, 0]
    offset_x = offset // total_y
    offset_y = offset % total_y
    inner_x = offset_x % rows_x
    inner_y = offset_y % cols_y
    carry_x = (point // cols_y < inner_x).astype(jnp.int32)
    carry_y = (point % cols_y < inner_y).astype(jnp.int32)
    shifts = jnp.stack(
        [offset_x // rows_x + carry_x, offset_y // cols_y + carry_y, inner_x, inner_y], axis=1
    )

    spread = lax.all_to_all(wannier.reshape(devices, rows, width), AXES, 0, 0, tiled=True)
    halves = half_turns(
        wannier.reshape(n_k, nb, width), coupling.reshape(n_q, n_k, modes, nb, width)
    )
    outgoing = shuffle(shifts, spread.reshape(count_x, count_y, rows, width), n_q)
    back = lax.all_to_all(outgoing.reshape(devices, n_q * rows, width), AXES, 0, 0, tiled=True)
    partner = back.reshape(n_k, pieces, n_q * rows, width)
    rotated = rotate(shifts, partner, halves, rows_x, cols_y)
    return rotated.reshape(coupling.shape)


def solution(mesh):
    in_specs = (P("kx", "ky", None, None), P(None, "kx", "ky", None, None, None), P())
    out_specs = P(None, "kx", "ky", None, None, None)
    return jax.shard_map(
        per_device, mesh=mesh, in_specs=in_specs, out_specs=out_specs, check_vma=False
    )
```

time: 345 us -> 67.1 us (0.19)
  waiting for transfers between devices: 241 us -> 27.6 us
  matrix products: 51.8 us -> 0 us
  Pallas kernels: 0 us -> 21.5 us
  between operations: 21 us -> 0.07 us
  other arithmetic: 20.9 us -> 1.49 us
  starting transfers between devices: 0.3 us -> 16.2 us
  local copies, waits for them, and re-layouts: 9.41 us -> 0 us
    all_gather x4 -> x0, waiting for transfers between devices: 240 us -> none  [the longest x3 189 us: per_device(): pick_segment = lax.all_gather(row_aligned, 'ky', axis=1, tiled=True)]
    dot_general x12 -> x0, matrix products: 51.8 us -> none  [the longest x3 14.2 us: per_device(): jnp.einsum('rj,xjab->xrab', pick_chooser, pick_segment, preferred_element...]
    all_to_all x0 -> x2, waiting for transfers between devices: none -> 27.6 us  [the longest x1 15.7 us: per_device(): lax.all_to_all(outgoing.reshape(devices, n_q * rows, width), AXES, 0, 0,...]
    pallas_call x0 -> x3, Pallas kernels: none -> 21.5 us  [the longest x1 10.7 us: rotate(): pl.pallas_call(lambda *refs: rotate_kernel(*refs, n_x=n_x, n_y=n_y), in_s...]
    all_to_all x0 -> x2, starting transfers between devices: none -> 16.2 us  [the longest x1 11.5 us: per_device(): lax.all_to_all(wannier.reshape(devices, rows, width), AXES, 0, 0, tiled=T...]
    slice x3 -> x0, other arithmetic: 11.5 us -> none  [rotate(): half_turn[..., half_width:]]
    another operation x1, other arithmetic: 8.51 us -> 0.08 us  [per_device(): jnp.stack([offset_x // rows_x + carry_x, offset_y // cols_y + carry_y, in...]
    slice x4 -> x0, local copies, waits for them, and re-layouts: 3.89 us -> none  [the longest x3 2.56 us: rotate(): partner[..., :half_width]]
  transfers between devices with their start and end apart: 4 -> 2, of which waited for: 4 -> 2; matrix products, arithmetic and copies ran while one was open for 14% -> 2% of each run, Pallas kernels for 0% -> 13%
where the time goes in v1:
time: 67.1 us; the launch traced here: 66.8 us
  waiting for transfers between devices  27.6 us (41%)
  Pallas kernels  21.5 us (32%)
  starting transfers between devices  16.2 us (24%)
  other arithmetic  1.49 us (2%)
    all_to_all x1, waiting for transfers between devices, per_device(): lax.all_to_all(outgoing.reshape(devices, n_q * rows, width), AXES, 0, 0,...  15.7 us
    all_to_all x1, waiting for transfers between devices, per_device(): lax.all_to_all(wannier.reshape(devices, rows, width), AXES, 0, 0, tiled=T...  11.9 us
    all_to_all x1, starting transfers between devices, per_device(): lax.all_to_all(wannier.reshape(devices, rows, width), AXES, 0, 0, tiled=T...  11.5 us
    pallas_call x1, Pallas kernels, rotate(): pl.pallas_call(lambda *refs: rotate_kernel(*refs, n_x=n_x, n_y=n_y), in_s...  10.7 us
    pallas_call x1, Pallas kernels, half_turns(): pl.pallas_call(half_turn_kernel, in_specs=[pl.BlockSpec(memory_space=pltp...  8.65 us
    all_to_all x1, starting transfers between devices, per_device(): lax.all_to_all(outgoing.reshape(devices, n_q * rows, width), AXES, 0, 0,...  4.67 us
    pallas_call x1, Pallas kernels, shuffle(): pl.pallas_call(shuffle_kernel, in_specs=[pl.BlockSpec(memory_space=pltpu....  2.17 us
  transfers between devices with their start and end apart: 2, of which 2 were waited for; matrix products, arithmetic and copies ran while one was open for 2% of the time, Pallas kernels for 13%

profile of v1, /device:TPU:1, one launch (start us, length us, event | category | flops | bytes accessed | tf_op | source)
XLA Modules:
  0.0 66.8 jit_solution(8843074966678133725)
XLA Ops:
  0.0 11.5 %all-to-all-start = ((bf16[128,16,128]{2,1,0:T(8,128)(2,1)}), bf16[128,16,128]{2,1,0:T(8,128)(2,1)S(1)}, u32[]{:S(2)}, u32[]{:S(2)}) async-start(bf16[128,16,128]{2,1,0:T(8,128)(2,1)} %bitcast.10), calls=%async_computation | async-start | bytes 1048576 | tf_op jit(solution)/shard_map/all_to_all | solution.py:196
  11.5 0.7 %fusion = (s32[3,1]{1,0:T(4,128)S(1)}, pred[3,1]{1,0:T(4,128)(4,1)S(1)}) fusion(s32[]{:T(128)S(6)} %select_n.52, s32[3,4096]{1,0:T(4,128)} %param.5), kind=kLoop, calls=%fused_computation.15 | loop fusion | flops 111 | bytes 31 | tf_op jit(solution)/shard_map/add | solution.py:193
  12.2 0.7 %fusion.1 = (s32[3,1]{1,0:T(4,128)S(1)}, s32[3,1]{1,0:T(4,128)S(1)}, s32[3,1]{1,0:T(4,128)S(1)}) fusion(s32[]{:T(128)S(6)} %select_n.56, pred[3,1]{1,0:T(4,128)(4,1)S(1)} %get-tuple-element.6, s32[3,4096]{1,0:T(4,128)} %param.5), kind=kLoop, calls=%fused_computation.16 | loop fusion | flops 153 | bytes 55 | tf_op jit(solution)/shard_map/add | solution.py:193
  12.9 0.1 pad_add_fusion.shift_ref.refs_0_
  13.0 11.9 %all-to-all-done = bf16[128,16,128]{2,1,0:T(8,128)(2,1)S(1)} async-done(((bf16[128,16,128]{2,1,0:T(8,128)(2,1)}), bf16[128,16,128]{2,1,0:T(8,128)(2,1)S(1)}, u32[]{:S(2)}, u32[]{:S(2)}) %all-to-all-start) | async-done | bytes 524320 | tf_op jit(solution)/shard_map/all_to_all | solution.py:196
  24.9 2.2 %shuffle.1 = bf16[8,16,48,128]{3,2,1,0:T(8,128)(2,1)} custom-call(s32[3,4]{1,0:T(4,128)S(1)} %pad_add_fusion.shift_ref.refs_0_, bf16[8,16,16,128]{3,2,1,0:T(8,128)(2,1)S(1)} %bitcast.8), custom_call_target="tpu_custom_call" | custom-call | tf_op jit(solution)/shard_map/shuffle/pallas_call | solution.py:106
  27.1 4.7 %all-to-all-start.1 = ((bf16[128,48,128]{2,1,0:T(8,128)(2,1)}), bf16[128,48,128]{2,1,0:T(8,128)(2,1)S(1)}, u32[]{:S(2)}, u32[]{:S(2)}) async-start(bf16[128,48,128]{2,1,0:T(8,128)(2,1)} %bitcast.2), calls=%async_computation.1 | async-start | bytes 3145728 | tf_op jit(solution)/shard_map/all_to_all | solution.py:201
  31.7 8.6 %half_turns.1.refs_2_ = bf16[3,32,3,128,128]{4,3,2,1,0:T(8,128)(2,1)} custom-call(bf16[32,64,128]{2,1,0:T(8,128)(2,1)} %bitcast.11, bf16[3,32,6,64,128]{4,3,2,1,0:T(8,128)(2,1)} %bitcast.9), custom_call_target="tpu_custom_call" | custom-call | flops 2415919104 | bytes 18874368 | tf_op jit(solution)/shard_map/half_turns/pallas_call | solution.py:77
  40.4 15.7 %all-to-all-done.1 = bf16[128,48,128]{2,1,0:T(8,128)(2,1)S(1)} async-done(((bf16[128,48,128]{2,1,0:T(8,128)(2,1)}), bf16[128,48,128]{2,1,0:T(8,128)(2,1)S(1)}, u32[]{:S(2)}, u32[]{:S(2)}) %all-to-all-start.1) | async-done | bytes 1572896 | tf_op jit(solution)/shard_map/all_to_all | solution.py:201
  56.1 10.7 %rotate.1 = bf16[3,32,6,64,128]{4,3,2,1,0:T(8,128)(2,1)} custom-call(s32[3,4]{1,0:T(4,128)S(1)} %pad_add_fusion.shift_ref.refs_0_, bf16[32,4,48,128]{3,2,1,0:T(8,128)(2,1)S(1)} %bitcast.7, bf16[3,32,3,128,128]{4,3,2,1,0:T(8,128)(2,1)} %half_turns.1.refs_2_), custom_call_target="tpu_custom_call" | custom-call | flops 1207959552 | bytes 18874368 | tf_op jit(solution)/shard_map/rotate/pallas_call | solution.py:152
Async XLA Ops:
  0.0 24.9 %all-to-all-start = ((bf16[128,16,128]{2,1,0:T(8,128)(2,1)}), bf16[128,16,128]{2,1,0:T(8,128)(2,1)S(1)}, u32[]{:S(2)}, u32[]{:S(2)}) async-start(bf16[128,16,128]{2,1,0:T(8,128)(2,1)} %bitcast.10), calls=%async_computation | async-start | bytes 1048576 | tf_op jit(solution)/shard_map/all_to_all | solution.py:196
  27.1 29.0 %all-to-all-start.1 = ((bf16[128,48,128]{2,1,0:T(8,128)(2,1)}), bf16[128,48,128]{2,1,0:T(8,128)(2,1)S(1)}, u32[]{:S(2)}, u32[]{:S(2)}) async-start(bf16[128,48,128]{2,1,0:T(8,128)(2,1)} %bitcast.2), calls=%async_computation.1 | async-start | bytes 3145728 | tf_op jit(solution)/shard_map/all_to_all | solution.py:201

commit v2 on v1

--- a/solution.py
+++ b/solution.py
@@ -65,15 +65,15 @@
             for p in range(modes // 2):
                 one = half[2 * p * nb : (2 * p + 1) * nb]
                 two = half[(2 * p + 1) * nb : (2 * p + 2) * nb]
-                o_buf[q, k, p, :nb] = jnp.concatenate([one[:, :nb], two[:, :nb]], axis=1)
-                o_buf[q, k, p, nb:] = jnp.concatenate([one[:, nb:], two[:, nb:]], axis=1)
+                o_buf[q, k, :nb, p * width : (p + 1) * width] = jnp.concatenate([one[:, :nb], two[:, :nb]], axis=1)
+                o_buf[q, k, nb:, p * width : (p + 1) * width] = jnp.concatenate([one[:, nb:], two[:, nb:]], axis=1)
 
     stream(g_ref, o_ref, g_buf, o_buf, in_sem, out_sem, work)
 
 
 def half_turns(wannier, coupling):
     n_q, n_k, modes, nb, width = coupling.shape
-    paired = (n_q, n_k, modes // 2, 2 * nb, width)
+    paired = (n_q, n_k, 2 * nb, modes // 2 * width)
     return pl.pallas_call(
         half_turn_kernel,
         in_specs=[pl.BlockSpec(memory_space=pltpu.VMEM), pl.BlockSpec(memory_space=pltpu.HBM)],
@@ -116,14 +116,29 @@
     )(shifts, held)
 
 
-def rotate_kernel(shift_ref, v_ref, h_ref, o_ref, h_buf, o_buf, in_sem, out_sem, *, n_x, n_y):
-    n_q, _, modes, nb, width = o_buf.shape
+def rotate_kernel(
+    shift_ref, v_ref, h_ref, o_ref, h_buf, o_buf, in_sem, out_sem, left_a, left_b, raw_a, raw_b, *, n_x, n_y
+):
+    n_q, n_k, modes, nb, width = o_buf.shape
     rows = v_ref.shape[2] // n_q
-
-    def work(k):
-        for q in range(n_q):
-            at_x = lax.rem(k // n_y + shift_ref[q, 2], n_x)
-            at_y = lax.rem(lax.rem(k, n_y) + shift_ref[q, 3], n_y)
+    pairs = modes // 2
+    groups = in_sem.shape[0]
+    size = n_k // groups
+    units = [(q, k) for k in range(size) for q in range(n_q)]
+
+    def fetch(i):
+        at = pl.ds(i * size, size)
+        return pltpu.make_async_copy(h_ref.at[:, at], h_buf.at[:, at], in_sem.at[i])
+
+    def send(i):
+        at = pl.ds(i * size, size)
+        return pltpu.make_async_copy(o_buf.at[:, at], o_ref.at[:, at], out_sem.at[i])
+
+    def prepare(i, left_ref):
+        for u, (q, k) in enumerate(units):
+            at = i * size + k
+            at_x = lax.rem(at // n_y + shift_ref[q, 2], n_x)
+            at_y = lax.rem(lax.rem(at, n_y) + shift_ref[q, 3], n_y)
             v = v_ref[at_x * n_y + at_y, :, q * rows : (q + 1) * rows].reshape(nb, width)
             left = jnp.concatenate(
                 [
@@ -132,22 +147,68 @@
                 ],
                 axis=0,
             )
-            right = jnp.concatenate([h_buf[q, k, p] for p in range(modes // 2)], axis=1)
-            out = lax.dot_general(
-                left, right, (((0,), (0,)), ((), ())), preferred_element_type=jnp.float32
-            ).astype(jnp.bfloat16)
-            for p in range(modes // 2):
-                real = out[:nb, p * width : (p + 1) * width]
-                imag = out[nb:, p * width : (p + 1) * width]
-                o_buf[q, k, 2 * p] = jnp.concatenate([real[:, :nb], imag[:, :nb]], axis=1)
-                o_buf[q, k, 2 * p + 1] = jnp.concatenate([real[:, nb:], imag[:, nb:]], axis=1)
-
-    stream(h_ref, o_ref, h_buf, o_buf, in_sem, out_sem, work)
+            left_ref[u] = left.T
+
+    def multiply(i, left_ref, raw_ref):
+        for u, (q, k) in enumerate(units):
+            right = h_buf[q, i * size + k]
+            out = jnp.dot(left_ref[u], right, preferred_element_type=jnp.float32)
+            raw_ref[u] = out
+
+    lane = lax.broadcasted_iota(jnp.int32, (nb, width), 1)
+
+    def arrange(i, raw_ref):
+        for u, (q, k) in enumerate(units):
+            at = i * size + k
+            for p in range(pairs):
+                real = raw_ref[u, :nb, p * width : (p + 1) * width]
+                imag = raw_ref[u, nb:, p * width : (p + 1) * width]
+                outer = jnp.where(lane < nb, real, imag)
+                inner = pltpu.roll(jnp.where(lane < nb, imag, real), nb, 1)
+                one = jnp.where(lane < nb, outer, inner)
+                two = jnp.where(lane < nb, inner, outer)
+                o_buf[q, at, 2 * p] = one.astype(jnp.bfloat16)
+                o_buf[q, at, 2 * p + 1] = two.astype(jnp.bfloat16)
+
+    def start(i, carry):
+        fetch(i).start()
+        return carry
+
+    def step(j, carry):
+        i = 2 * j
+        last = jnp.maximum(i - 1, 0)
+        fetch(i).wait()
+        multiply(i, left_a, raw_a)
+        prepare(i + 1, left_b)
+        arrange(last, raw_b)
+
+        @pl.when(j > 0)
+        def _():
+            send(last).start()
+
+        fetch(i + 1).wait()
+        multiply(i + 1, left_b, raw_b)
+        prepare(jnp.minimum(i + 2, groups - 1), left_a)
+        arrange(i, raw_a)
+        send(i).start()
+        return carry
+
+    def finish(i, carry):
+        send(i).wait()
+        return carry
+
+    lax.fori_loop(0, groups, start, 0)
+    prepare(0, left_a)
+    lax.fori_loop(0, groups // 2, step, 0)
+    arrange(groups - 1, raw_b)
+    send(groups - 1).start()
+    lax.fori_loop(0, groups, finish, 0)
 
 
 def rotate(shifts, partner, halves, n_x, n_y):
-    n_q, n_k, pairs, _, width = halves.shape
-    modes, nb = 2 * pairs, width // 2
+    n_q, n_k, width, columns = halves.shape
+    pairs, nb = columns // width, width // 2
+    modes = 2 * pairs
     shape = (n_q, n_k, modes, nb, width)
     return pl.pallas_call(
         lambda *refs: rotate_kernel(*refs, n_x=n_x, n_y=n_y),
@@ -158,7 +219,9 @@
         ],
         out_specs=pl.BlockSpec(memory_space=pltpu.HBM),
         out_shape=jax.ShapeDtypeStruct(shape, jnp.bfloat16),
-        scratch_shapes=stream_scratch(halves.shape, shape, R_GROUPS),
+        scratch_shapes=stream_scratch(halves.shape, shape, R_GROUPS)
+        + [pltpu.VMEM((n_k // R_GROUPS * n_q, width, width), jnp.bfloat16)] * 2
+        + [pltpu.VMEM((n_k // R_GROUPS * n_q, width, pairs * width), jnp.float32)] * 2,
         compiler_params=pltpu.CompilerParams(vmem_limit_bytes=50 * MIB),
         cost_estimate=pl.CostEstimate(
             flops=4 * n_q * n_k * modes * nb * width * nb,

time: 67.1 us -> 65 us (0.969)
  Pallas kernels: 21.5 us -> 19.5 us
    pallas_call x1, Pallas kernels: 10.7 us -> 8.65 us  [rotate(): pl.pallas_call(lambda *refs: rotate_kernel(*refs, n_x=n_x, n_y=n_y), in_s...]
where the time goes in v2:
time: 65 us; the launch traced here: 64.7 us
  waiting for transfers between devices  27.6 us (42%)
  Pallas kernels  19.5 us (30%)
  starting transfers between devices  16.2 us (25%)
  other arithmetic  1.49 us (2%)
    all_to_all x1, waiting for transfers between devices, per_device(): lax.all_to_all(outgoing.reshape(devices, n_q * rows, width), AXES, 0, 0,...  15.7 us
    all_to_all x1, waiting for transfers between devices, per_device(): lax.all_to_all(wannier.reshape(devices, rows, width), AXES, 0, 0, tiled=T...  11.9 us
    all_to_all x1, starting transfers between devices, per_device(): lax.all_to_all(wannier.reshape(devices, rows, width), AXES, 0, 0, tiled=T...  11.5 us
    pallas_call x1, Pallas kernels, rotate(): pl.pallas_call(lambda *refs: rotate_kernel(*refs, n_x=n_x, n_y=n_y), in_s...  8.65 us
    pallas_call x1, Pallas kernels, half_turns(): pl.pallas_call(half_turn_kernel, in_specs=[pl.BlockSpec(memory_space=pltp...  8.65 us
    all_to_all x1, starting transfers between devices, per_device(): lax.all_to_all(outgoing.reshape(devices, n_q * rows, width), AXES, 0, 0,...  4.67 us
    pallas_call x1, Pallas kernels, shuffle(): pl.pallas_call(shuffle_kernel, in_specs=[pl.BlockSpec(memory_space=pltpu....  2.17 us
  transfers between devices with their start and end apart: 2, of which 2 were waited for; matrix products, arithmetic and copies ran while one was open for 2% of the time, Pallas kernels for 13%

profile of v2, /device:TPU:1, one launch (start us, length us, event | category | flops | bytes accessed | tf_op | source)
XLA Modules:
  0.0 64.7 jit_solution(12371864976879651579)
XLA Ops:
  0.0 11.5 %all-to-all-start = ((bf16[128,16,128]{2,1,0:T(8,128)(2,1)}), bf16[128,16,128]{2,1,0:T(8,128)(2,1)S(1)}, u32[]{:S(2)}, u32[]{:S(2)}) async-start(bf16[128,16,128]{2,1,0:T(8,128)(2,1)} %bitcast.10), calls=%async_computation | async-start | bytes 1048576 | tf_op jit(solution)/shard_map/all_to_all | solution.py:259
  11.5 0.7 %fusion = (s32[3,1]{1,0:T(4,128)S(1)}, pred[3,1]{1,0:T(4,128)(4,1)S(1)}) fusion(s32[]{:T(128)S(6)} %select_n.52, s32[3,4096]{1,0:T(4,128)} %param.5), kind=kLoop, calls=%fused_computation.15 | loop fusion | flops 111 | bytes 31 | tf_op jit(solution)/shard_map/add | solution.py:256
  12.2 0.7 %fusion.1 = (s32[3,1]{1,0:T(4,128)S(1)}, s32[3,1]{1,0:T(4,128)S(1)}, s32[3,1]{1,0:T(4,128)S(1)}) fusion(s32[]{:T(128)S(6)} %select_n.56, pred[3,1]{1,0:T(4,128)(4,1)S(1)} %get-tuple-element.6, s32[3,4096]{1,0:T(4,128)} %param.5), kind=kLoop, calls=%fused_computation.16 | loop fusion | flops 153 | bytes 55 | tf_op jit(solution)/shard_map/add | solution.py:256
  12.9 0.1 pad_add_fusion.shift_ref.refs_0_
  13.0 11.9 %all-to-all-done = bf16[128,16,128]{2,1,0:T(8,128)(2,1)S(1)} async-done(((bf16[128,16,128]{2,1,0:T(8,128)(2,1)}), bf16[128,16,128]{2,1,0:T(8,128)(2,1)S(1)}, u32[]{:S(2)}, u32[]{:S(2)}) %all-to-all-start) | async-done | bytes 524320 | tf_op jit(solution)/shard_map/all_to_all | solution.py:259
  24.9 2.2 %shuffle.1 = bf16[8,16,48,128]{3,2,1,0:T(8,128)(2,1)} custom-call(s32[3,4]{1,0:T(4,128)S(1)} %pad_add_fusion.shift_ref.refs_0_, bf16[8,16,16,128]{3,2,1,0:T(8,128)(2,1)S(1)} %bitcast.8), custom_call_target="tpu_custom_call" | custom-call | tf_op jit(solution)/shard_map/shuffle/pallas_call | solution.py:106
  27.1 4.7 %all-to-all-start.1 = ((bf16[128,48,128]{2,1,0:T(8,128)(2,1)}), bf16[128,48,128]{2,1,0:T(8,128)(2,1)S(1)}, u32[]{:S(2)}, u32[]{:S(2)}) async-start(bf16[128,48,128]{2,1,0:T(8,128)(2,1)} %bitcast.2), calls=%async_computation.1 | async-start | bytes 3145728 | tf_op jit(solution)/shard_map/all_to_all | solution.py:264
  31.7 8.6 %half_turns.1.refs_2_ = bf16[3,32,128,384]{3,2,1,0:T(8,128)(2,1)} custom-call(bf16[32,64,128]{2,1,0:T(8,128)(2,1)} %bitcast.11, bf16[3,32,6,64,128]{4,3,2,1,0:T(8,128)(2,1)} %bitcast.9), custom_call_target="tpu_custom_call" | custom-call | flops 2415919104 | bytes 18874368 | tf_op jit(solution)/shard_map/half_turns/pallas_call | solution.py:77
  40.4 15.7 %all-to-all-done.1 = bf16[128,48,128]{2,1,0:T(8,128)(2,1)S(1)} async-done(((bf16[128,48,128]{2,1,0:T(8,128)(2,1)}), bf16[128,48,128]{2,1,0:T(8,128)(2,1)S(1)}, u32[]{:S(2)}, u32[]{:S(2)}) %all-to-all-start.1) | async-done | bytes 1572896 | tf_op jit(solution)/shard_map/all_to_all | solution.py:264
  56.1 8.7 %rotate.1 = bf16[3,32,6,64,128]{4,3,2,1,0:T(8,128)(2,1)} custom-call(s32[3,4]{1,0:T(4,128)S(1)} %pad_add_fusion.shift_ref.refs_0_, bf16[32,4,48,128]{3,2,1,0:T(8,128)(2,1)S(1)} %bitcast.7, bf16[3,32,128,384]{3,2,1,0:T(8,128)(2,1)} %half_turns.1.refs_2_), custom_call_target="tpu_custom_call" | custom-call | flops 1207959552 | bytes 18874368 | tf_op jit(solution)/shard_map/rotate/pallas_call | solution.py:213
Async XLA Ops:
  0.0 24.9 %all-to-all-start = ((bf16[128,16,128]{2,1,0:T(8,128)(2,1)}), bf16[128,16,128]{2,1,0:T(8,128)(2,1)S(1)}, u32[]{:S(2)}, u32[]{:S(2)}) async-start(bf16[128,16,128]{2,1,0:T(8,128)(2,1)} %bitcast.10), calls=%async_computation | async-start | bytes 1048576 | tf_op jit(solution)/shard_map/all_to_all | solution.py:259
  27.1 29.0 %all-to-all-start.1 = ((bf16[128,48,128]{2,1,0:T(8,128)(2,1)}), bf16[128,48,128]{2,1,0:T(8,128)(2,1)S(1)}, u32[]{:S(2)}, u32[]{:S(2)}) async-start(bf16[128,48,128]{2,1,0:T(8,128)(2,1)} %bitcast.2), calls=%async_computation.1 | async-start | bytes 3145728 | tf_op jit(solution)/shard_map/all_to_all | solution.py:264

commit v3 on v2

--- a/solution.py
+++ b/solution.py
@@ -1,11 +1,16 @@
 import jax
 import jax.numpy as jnp
+import numpy as np
 from jax import lax
 from jax.experimental import pallas as pl
 from jax.experimental.pallas import tpu as pltpu
 from jax.sharding import PartitionSpec as P
 
-AXES = ("kx", "ky")
+X_AXES = ("z_lo", "y")
+Y_AXES = ("x", "z_hi", "core")
+X_SIZES = (2, 4)
+Y_SIZES = (4, 2, 2)
+ORDER = ("core", "z_hi", "z_lo", "x", "y")
 MIB = 1024 * 1024
 H_GROUPS = 8
 R_GROUPS = 16
@@ -90,19 +95,38 @@
     )(wannier, coupling)
 
 
-def shuffle_kernel(shift_ref, held_ref, o_ref):
-    n_x, n_y, rows, _ = held_ref.shape
-    for q in range(o_ref.shape[2] // rows):
+def grid_places():
+    sizes = dict(zip(X_AXES + Y_AXES, X_SIZES + Y_SIZES))
+    places = []
+    for at in np.ndindex(*(sizes[name] for name in ORDER)):
+        where = dict(zip(ORDER, at))
+        x = np.ravel_multi_index([where[name] for name in X_AXES], X_SIZES)
+        y = np.ravel_multi_index([where[name] for name in Y_AXES], Y_SIZES)
+        places.append((int(x), int(y)))
+    return places
+
+
+def shuffle_kernel(shift_ref, held_ref, o_ref, twice_ref):
+    n_x = twice_ref.shape[0]
+    n_y = twice_ref.shape[1] // 2
+    rows = held_ref.shape[1]
+    number = {}
+    for at, (x, y) in enumerate(grid_places()):
+        number[x, y] = at
+        tile = held_ref[at]
+        twice_ref[x, y] = tile
+        twice_ref[x, n_y + y] = tile
+    for q in range(o_ref.shape[1] // rows):
         shift_x = shift_ref[q, 0]
-        shift_y = shift_ref[q, 1]
-        for y in range(n_y):
-            from_y = lax.rem(shift_y + y, n_y)
-            for x in range(n_x):
-                o_ref[x, y, q * rows : (q + 1) * rows] = held_ref[lax.rem(shift_x + x, n_x), from_y]
-
-
-def shuffle(shifts, held, n_q):
-    n_x, n_y, rows, width = held.shape
+        run = pl.ds(lax.rem(shift_ref[q, 1], n_y), n_y)
+        for x in range(n_x):
+            row = twice_ref[lax.rem(shift_x + x, n_x), run]
+            for y in range(n_y):
+                o_ref[number[x, y], q * rows : (q + 1) * rows] = row[y]
+
+
+def shuffle(shifts, held, n_x, n_y, n_q):
+    devices, rows, width = held.shape
     return pl.pallas_call(
         shuffle_kernel,
         in_specs=[
@@ -110,7 +134,8 @@
             pl.BlockSpec(memory_space=pltpu.VMEM),
         ],
         out_specs=pl.BlockSpec(memory_space=pltpu.VMEM),
-        out_shape=jax.ShapeDtypeStruct((n_x, n_y, n_q * rows, width), held.dtype),
+        out_shape=jax.ShapeDtypeStruct((devices, n_q * rows, width), held.dtype),
+        scratch_shapes=[pltpu.VMEM((n_x, 2 * n_y, rows, width), held.dtype)],
         compiler_params=pltpu.CompilerParams(vmem_limit_bytes=8 * MIB),
         name="shuffle",
     )(shifts, held)
@@ -236,14 +261,14 @@
     rows_x, cols_y, nb, width = wannier.shape
     n_q = coupling.shape[0]
     modes = coupling.shape[3]
-    count_x = lax.axis_size("kx")
-    count_y = lax.axis_size("ky")
+    count_x = lax.axis_size(X_AXES)
+    count_y = lax.axis_size(Y_AXES)
     devices = count_x * count_y
     n_k = rows_x * cols_y
     pieces = devices // n_k
     rows = nb // pieces
     total_y = cols_y * count_y
-    me = lax.axis_index("kx") * count_y + lax.axis_index("ky")
+    me = lax.axis_index(ORDER)
     point = me // pieces
     offset = kq_map[:, 0]
     offset_x = offset // total_y
@@ -256,20 +281,23 @@
         [offset_x // rows_x + carry_x, offset_y // cols_y + carry_y, inner_x, inner_y], axis=1
     )
 
-    spread = lax.all_to_all(wannier.reshape(devices, rows, width), AXES, 0, 0, tiled=True)
+    spread = lax.all_to_all(wannier.reshape(devices, rows, width), ORDER, 0, 0, tiled=True)
     halves = half_turns(
         wannier.reshape(n_k, nb, width), coupling.reshape(n_q, n_k, modes, nb, width)
     )
-    outgoing = shuffle(shifts, spread.reshape(count_x, count_y, rows, width), n_q)
-    back = lax.all_to_all(outgoing.reshape(devices, n_q * rows, width), AXES, 0, 0, tiled=True)
+    outgoing = shuffle(shifts, spread, count_x, count_y, n_q)
+    back = lax.all_to_all(outgoing, ORDER, 0, 0, tiled=True)
     partner = back.reshape(n_k, pieces, n_q * rows, width)
     rotated = rotate(shifts, partner, halves, rows_x, cols_y)
     return rotated.reshape(coupling.shape)
 
 
 def solution(mesh):
-    in_specs = (P("kx", "ky", None, None), P(None, "kx", "ky", None, None, None), P())
-    out_specs = P(None, "kx", "ky", None, None, None)
+    links = jax.sharding.Mesh(
+        mesh.devices.reshape(X_SIZES + Y_SIZES), X_AXES + Y_AXES, axis_types=mesh.axis_types[:1] * 5
+    )
+    in_specs = (P(X_AXES, Y_AXES), P(None, X_AXES, Y_AXES), P())
+    out_specs = P(None, X_AXES, Y_AXES)
     return jax.shard_map(
-        per_device, mesh=mesh, in_specs=in_specs, out_specs=out_specs, check_vma=False
+        per_device, mesh=links, in_specs=in_specs, out_specs=out_specs, check_vma=False
     )

time: 65 us -> 63.1 us (0.971)
  waiting for transfers between devices: 27.6 us -> 25.6 us
    all_to_all x2, waiting for transfers between devices: 27.6 us -> 25.6 us  [the longest x1 14 us: per_device(): back = lax.all_to_all(outgoing, ORDER, 0, 0, tiled=True)]
  transfers between devices with their start and end apart: 2 -> 2, of which waited for: 2 -> 2; matrix products, arithmetic and copies ran while one was open for 2% -> 2% of each run, Pallas kernels for 13% -> 14%
where the time goes in v3:
time: 63.1 us; the launch traced here: 62.6 us
  waiting for transfers between devices  25.6 us (41%)
  Pallas kernels  19.3 us (31%)
  starting transfers between devices  16.2 us (26%)
  other arithmetic  1.49 us (2%)
    all_to_all x1, waiting for transfers between devices, per_device(): back = lax.all_to_all(outgoing, ORDER, 0, 0, tiled=True)  14 us
    all_to_all x1, waiting for transfers between devices, per_device(): lax.all_to_all(wannier.reshape(devices, rows, width), ORDER, 0, 0, tiled=...  11.5 us
    all_to_all x1, starting transfers between devices, per_device(): lax.all_to_all(wannier.reshape(devices, rows, width), ORDER, 0, 0, tiled=...  11.5 us
    pallas_call x1, Pallas kernels, rotate(): pl.pallas_call(lambda *refs: rotate_kernel(*refs, n_x=n_x, n_y=n_y), in_s...  8.65 us
    pallas_call x1, Pallas kernels, half_turns(): pl.pallas_call(half_turn_kernel, in_specs=[pl.BlockSpec(memory_space=pltp...  8.63 us
    all_to_all x1, starting transfers between devices, per_device(): back = lax.all_to_all(outgoing, ORDER, 0, 0, tiled=True)  4.67 us
    pallas_call x1, Pallas kernels, shuffle(): pl.pallas_call(shuffle_kernel, in_specs=[pl.BlockSpec(memory_space=pltpu....  2.04 us
  transfers between devices with their start and end apart: 2, of which 2 were waited for; matrix products, arithmetic and copies ran while one was open for 2% of the time, Pallas kernels for 14%

profile of v3, /device:TPU:1, one launch (start us, length us, event | category | flops | bytes accessed | tf_op | source)
XLA Modules:
  0.0 62.6 jit_solution(6110237111975929255)
XLA Ops:
  0.0 11.5 %all-to-all-start = ((bf16[128,16,128]{2,1,0:T(8,128)(2,1)}), bf16[128,16,128]{2,1,0:T(8,128)(2,1)S(1)}, u32[]{:S(2)}, u32[]{:S(2)}) async-start(bf16[128,16,128]{2,1,0:T(8,128)(2,1)} %bitcast.7), calls=%async_computation | async-start | bytes 1048576 | tf_op jit(solution)/shard_map/all_to_all | solution.py:284
  11.5 0.7 %fusion = (s32[3,1]{1,0:T(4,128)S(1)}, pred[3,1]{1,0:T(4,128)(4,1)S(1)}) fusion(s32[]{:T(128)S(6)} %select_n.52, s32[3,4096]{1,0:T(4,128)} %param.5), kind=kLoop, calls=%fused_computation.15 | loop fusion | flops 111 | bytes 31 | tf_op jit(solution)/shard_map/add | solution.py:281
  12.2 0.7 %fusion.1 = (s32[3,1]{1,0:T(4,128)S(1)}, s32[3,1]{1,0:T(4,128)S(1)}, s32[3,1]{1,0:T(4,128)S(1)}) fusion(s32[]{:T(128)S(6)} %select_n.56, pred[3,1]{1,0:T(4,128)(4,1)S(1)} %get-tuple-element.6, s32[3,4096]{1,0:T(4,128)} %param.5), kind=kLoop, calls=%fused_computation.16 | loop fusion | flops 153 | bytes 55 | tf_op jit(solution)/shard_map/add | solution.py:281
  13.0 0.1 pad_add_fusion.shift_ref.refs_0_
  13.0 11.5 %all-to-all-done.held_ref = bf16[128,16,128]{2,1,0:T(8,128)(2,1)S(1)} async-done(((bf16[128,16,128]{2,1,0:T(8,128)(2,1)}), bf16[128,16,128]{2,1,0:T(8,128)(2,1)S(1)}, u32[]{:S(2)}, u32[]{:S(2)}) %all-to-all-start) | async-done | bytes 524320 | tf_op jit(solution)/shard_map/all_to_all | solution.py:284
  24.6 2.0 %shuffle.1 = bf16[128,48,128]{2,1,0:T(8,128)(2,1)} custom-call(s32[3,4]{1,0:T(4,128)S(1)} %pad_add_fusion.shift_ref.refs_0_, bf16[128,16,128]{2,1,0:T(8,128)(2,1)S(1)} %all-to-all-done.held_ref), custom_call_target="tpu_custom_call" | custom-call | tf_op jit(solution)/shard_map/shuffle/pallas_call | solution.py:130
  26.6 4.7 %all-to-all-start.1 = ((bf16[128,48,128]{2,1,0:T(8,128)(2,1)}), bf16[128,48,128]{2,1,0:T(8,128)(2,1)S(1)}, u32[]{:S(2)}, u32[]{:S(2)}) async-start(bf16[128,48,128]{2,1,0:T(8,128)(2,1)} %shuffle.1), calls=%async_computation.1 | async-start | bytes 3145728 | tf_op jit(solution)/shard_map/all_to_all | solution.py:289
  31.3 8.6 %half_turns.1.refs_2_ = bf16[3,32,128,384]{3,2,1,0:T(8,128)(2,1)} custom-call(bf16[32,64,128]{2,1,0:T(8,128)(2,1)} %bitcast.8, bf16[3,32,6,64,128]{4,3,2,1,0:T(8,128)(2,1)} %bitcast.6), custom_call_target="tpu_custom_call" | custom-call | flops 2415919104 | bytes 18874368 | tf_op jit(solution)/shard_map/half_turns/pallas_call | solution.py:82
  39.9 14.0 %all-to-all-done.1 = bf16[128,48,128]{2,1,0:T(8,128)(2,1)S(1)} async-done(((bf16[128,48,128]{2,1,0:T(8,128)(2,1)}), bf16[128,48,128]{2,1,0:T(8,128)(2,1)S(1)}, u32[]{:S(2)}, u32[]{:S(2)}) %all-to-all-start.1) | async-done | bytes 1572896 | tf_op jit(solution)/shard_map/all_to_all | solution.py:289
  53.9 8.6 %rotate.1 = bf16[3,32,6,64,128]{4,3,2,1,0:T(8,128)(2,1)} custom-call(s32[3,4]{1,0:T(4,128)S(1)} %pad_add_fusion.shift_ref.refs_0_, bf16[32,4,48,128]{3,2,1,0:T(8,128)(2,1)S(1)} %bitcast.5, bf16[3,32,128,384]{3,2,1,0:T(8,128)(2,1)} %half_turns.1.refs_2_), custom_call_target="tpu_custom_call" | custom-call | flops 1207959552 | bytes 18874368 | tf_op jit(solution)/shard_map/rotate/pallas_call | solution.py:238
Async XLA Ops:
  0.0 24.6 %all-to-all-start = ((bf16[128,16,128]{2,1,0:T(8,128)(2,1)}), bf16[128,16,128]{2,1,0:T(8,128)(2,1)S(1)}, u32[]{:S(2)}, u32[]{:S(2)}) async-start(bf16[128,16,128]{2,1,0:T(8,128)(2,1)} %bitcast.7), calls=%async_computation | async-start | bytes 1048576 | tf_op jit(solution)/shard_map/all_to_all | solution.py:284
  26.6 27.3 %all-to-all-start.1 = ((bf16[128,48,128]{2,1,0:T(8,128)(2,1)}), bf16[128,48,128]{2,1,0:T(8,128)(2,1)S(1)}, u32[]{:S(2)}, u32[]{:S(2)}) async-start(bf16[128,48,128]{2,1,0:T(8,128)(2,1)} %shuffle.1), calls=%async_computation.1 | async-start | bytes 3145728 | tf_op jit(solution)/shard_map/all_to_all | solution.py:289

commit v4 on v3

--- a/solution.py
+++ b/solution.py
@@ -52,8 +52,8 @@
     return [
         pltpu.VMEM(shape_in, jnp.bfloat16),
         pltpu.VMEM(shape_out, jnp.bfloat16),
-        pltpu.SemaphoreType.DMA((groups,)),
-        pltpu.SemaphoreType.DMA((groups,)),
+        pltpu.SemaphoreType.DMA(groups),
+        pltpu.SemaphoreType.DMA(groups),
     ]
 
 
@@ -84,7 +84,7 @@
         in_specs=[pl.BlockSpec(memory_space=pltpu.VMEM), pl.BlockSpec(memory_space=pltpu.HBM)],
         out_specs=pl.BlockSpec(memory_space=pltpu.HBM),
         out_shape=jax.ShapeDtypeStruct(paired, jnp.bfloat16),
-        scratch_shapes=stream_scratch(coupling.shape, paired, H_GROUPS),
+        scratch_shapes=stream_scratch(coupling.shape, paired, (H_GROUPS,)),
         compiler_params=pltpu.CompilerParams(vmem_limit_bytes=56 * MIB),
         cost_estimate=pl.CostEstimate(
             flops=4 * n_q * n_k * modes * nb * width * width,
@@ -151,13 +151,17 @@
     size = n_k // groups
     units = [(q, k) for k in range(size) for q in range(n_q)]
 
-    def fetch(i):
+    def fetch(i, q):
         at = pl.ds(i * size, size)
-        return pltpu.make_async_copy(h_ref.at[:, at], h_buf.at[:, at], in_sem.at[i])
-
-    def send(i):
+        return pltpu.make_async_copy(h_ref.at[q, at], h_buf.at[q, at], in_sem.at[i, q])
+
+    def send(i, q):
         at = pl.ds(i * size, size)
-        return pltpu.make_async_copy(o_buf.at[:, at], o_ref.at[:, at], out_sem.at[i])
+        return pltpu.make_async_copy(o_buf.at[q, at], o_ref.at[q, at], out_sem.at[i, q])
+
+    def each(copy, i, action):
+        for q in range(n_q):
+            getattr(copy(i, q), action)()
 
     def prepare(i, left_ref):
         for u, (q, k) in enumerate(units):
@@ -196,37 +200,37 @@
                 o_buf[q, at, 2 * p + 1] = two.astype(jnp.bfloat16)
 
     def start(i, carry):
-        fetch(i).start()
+        each(fetch, i, "start")
         return carry
 
     def step(j, carry):
         i = 2 * j
         last = jnp.maximum(i - 1, 0)
-        fetch(i).wait()
+        each(fetch, i, "wait")
         multiply(i, left_a, raw_a)
         prepare(i + 1, left_b)
         arrange(last, raw_b)
 
         @pl.when(j > 0)
         def _():
-            send(last).start()
-
-        fetch(i + 1).wait()
+            each(send, last, "start")
+
+        each(fetch, i + 1, "wait")
         multiply(i + 1, left_b, raw_b)
         prepare(jnp.minimum(i + 2, groups - 1), left_a)
         arrange(i, raw_a)
-        send(i).start()
+        each(send, i, "start")
         return carry
 
     def finish(i, carry):
-        send(i).wait()
+        each(send, i, "wait")
         return carry
 
     lax.fori_loop(0, groups, start, 0)
     prepare(0, left_a)
     lax.fori_loop(0, groups // 2, step, 0)
     arrange(groups - 1, raw_b)
-    send(groups - 1).start()
+    each(send, groups - 1, "start")
     lax.fori_loop(0, groups, finish, 0)
 
 
@@ -244,7 +248,7 @@
         ],
         out_specs=pl.BlockSpec(memory_space=pltpu.HBM),
         out_shape=jax.ShapeDtypeStruct(shape, jnp.bfloat16),
-        scratch_shapes=stream_scratch(halves.shape, shape, R_GROUPS)
+        scratch_shapes=stream_scratch(halves.shape, shape, (R_GROUPS, n_q))
         + [pltpu.VMEM((n_k // R_GROUPS * n_q, width, width), jnp.bfloat16)] * 2
         + [pltpu.VMEM((n_k // R_GROUPS * n_q, width, pairs * width), jnp.float32)] * 2,
         compiler_params=pltpu.CompilerParams(vmem_limit_bytes=50 * MIB),

time: 63.1 us -> 63.8 us (1.011)
  Pallas kernels: 19.3 us -> 20 us
where the time goes in v4:
time: 63.8 us; the launch traced here: 63.2 us
  waiting for transfers between devices  25.6 us (40%)
  Pallas kernels  20 us (31%)
  starting transfers between devices  16.2 us (25%)
  other arithmetic  1.49 us (2%)
    all_to_all x1, waiting for transfers between devices, per_device(): back = lax.all_to_all(outgoing, ORDER, 0, 0, tiled=True)  14 us
    all_to_all x1, waiting for transfers between devices, per_device(): lax.all_to_all(wannier.reshape(devices, rows, width), ORDER, 0, 0, tiled=...  11.5 us
    all_to_all x1, starting transfers between devices, per_device(): lax.all_to_all(wannier.reshape(devices, rows, width), ORDER, 0, 0, tiled=...  11.5 us
    pallas_call x1, Pallas kernels, rotate(): pl.pallas_call(lambda *refs: rotate_kernel(*refs, n_x=n_x, n_y=n_y), in_s...  9.29 us
    pallas_call x1, Pallas kernels, half_turns(): pl.pallas_call(half_turn_kernel, in_specs=[pl.BlockSpec(memory_space=pltp...  8.63 us
    all_to_all x1, starting transfers between devices, per_device(): back = lax.all_to_all(outgoing, ORDER, 0, 0, tiled=True)  4.67 us
    pallas_call x1, Pallas kernels, shuffle(): pl.pallas_call(shuffle_kernel, in_specs=[pl.BlockSpec(memory_space=pltpu....  2.04 us
  transfers between devices with their start and end apart: 2, of which 2 were waited for; matrix products, arithmetic and copies ran while one was open for 2% of the time, Pallas kernels for 14%

profile of v4, /device:TPU:1, one launch (start us, length us, event | category | flops | bytes accessed | tf_op | source)
XLA Modules:
  0.0 63.2 jit_solution(13612311537165437297)
XLA Ops:
  0.0 11.5 %all-to-all-start = ((bf16[128,16,128]{2,1,0:T(8,128)(2,1)}), bf16[128,16,128]{2,1,0:T(8,128)(2,1)S(1)}, u32[]{:S(2)}, u32[]{:S(2)}) async-start(bf16[128,16,128]{2,1,0:T(8,128)(2,1)} %bitcast.7), calls=%async_computation | async-start | bytes 1048576 | tf_op jit(solution)/shard_map/all_to_all | solution.py:288
  11.5 0.7 %fusion = (s32[3,1]{1,0:T(4,128)S(1)}, pred[3,1]{1,0:T(4,128)(4,1)S(1)}) fusion(s32[]{:T(128)S(6)} %select_n.52, s32[3,4096]{1,0:T(4,128)} %param.5), kind=kLoop, calls=%fused_computation.15 | loop fusion | flops 111 | bytes 31 | tf_op jit(solution)/shard_map/add | solution.py:285
  12.2 0.7 %fusion.1 = (s32[3,1]{1,0:T(4,128)S(1)}, s32[3,1]{1,0:T(4,128)S(1)}, s32[3,1]{1,0:T(4,128)S(1)}) fusion(s32[]{:T(128)S(6)} %select_n.56, pred[3,1]{1,0:T(4,128)(4,1)S(1)} %get-tuple-element.6, s32[3,4096]{1,0:T(4,128)} %param.5), kind=kLoop, calls=%fused_computation.16 | loop fusion | flops 153 | bytes 55 | tf_op jit(solution)/shard_map/add | solution.py:285
  13.0 0.1 pad_add_fusion.shift_ref.refs_0_
  13.0 11.5 %all-to-all-done.held_ref = bf16[128,16,128]{2,1,0:T(8,128)(2,1)S(1)} async-done(((bf16[128,16,128]{2,1,0:T(8,128)(2,1)}), bf16[128,16,128]{2,1,0:T(8,128)(2,1)S(1)}, u32[]{:S(2)}, u32[]{:S(2)}) %all-to-all-start) | async-done | bytes 524320 | tf_op jit(solution)/shard_map/all_to_all | solution.py:288
  24.6 2.0 %shuffle.1 = bf16[128,48,128]{2,1,0:T(8,128)(2,1)} custom-call(s32[3,4]{1,0:T(4,128)S(1)} %pad_add_fusion.shift_ref.refs_0_, bf16[128,16,128]{2,1,0:T(8,128)(2,1)S(1)} %all-to-all-done.held_ref), custom_call_target="tpu_custom_call" | custom-call | tf_op jit(solution)/shard_map/shuffle/pallas_call | solution.py:130
  26.6 4.7 %all-to-all-start.1 = ((bf16[128,48,128]{2,1,0:T(8,128)(2,1)}), bf16[128,48,128]{2,1,0:T(8,128)(2,1)S(1)}, u32[]{:S(2)}, u32[]{:S(2)}) async-start(bf16[128,48,128]{2,1,0:T(8,128)(2,1)} %shuffle.1), calls=%async_computation.1 | async-start | bytes 3145728 | tf_op jit(solution)/shard_map/all_to_all | solution.py:293
  31.3 8.6 %half_turns.1.refs_2_ = bf16[3,32,128,384]{3,2,1,0:T(8,128)(2,1)} custom-call(bf16[32,64,128]{2,1,0:T(8,128)(2,1)} %bitcast.8, bf16[3,32,6,64,128]{4,3,2,1,0:T(8,128)(2,1)} %bitcast.6), custom_call_target="tpu_custom_call" | custom-call | flops 2415919104 | bytes 18874368 | tf_op jit(solution)/shard_map/half_turns/pallas_call | solution.py:82
  39.9 14.0 %all-to-all-done.1 = bf16[128,48,128]{2,1,0:T(8,128)(2,1)S(1)} async-done(((bf16[128,48,128]{2,1,0:T(8,128)(2,1)}), bf16[128,48,128]{2,1,0:T(8,128)(2,1)S(1)}, u32[]{:S(2)}, u32[]{:S(2)}) %all-to-all-start.1) | async-done | bytes 1572896 | tf_op jit(solution)/shard_map/all_to_all | solution.py:293
  53.9 9.3 %rotate.1 = bf16[3,32,6,64,128]{4,3,2,1,0:T(8,128)(2,1)} custom-call(s32[3,4]{1,0:T(4,128)S(1)} %pad_add_fusion.shift_ref.refs_0_, bf16[32,4,48,128]{3,2,1,0:T(8,128)(2,1)S(1)} %bitcast.5, bf16[3,32,128,384]{3,2,1,0:T(8,128)(2,1)} %half_turns.1.refs_2_), custom_call_target="tpu_custom_call" | custom-call | flops 1207959552 | bytes 18874368 | tf_op jit(solution)/shard_map/rotate/pallas_call | solution.py:242
Async XLA Ops:
  0.0 24.6 %all-to-all-start = ((bf16[128,16,128]{2,1,0:T(8,128)(2,1)}), bf16[128,16,128]{2,1,0:T(8,128)(2,1)S(1)}, u32[]{:S(2)}, u32[]{:S(2)}) async-start(bf16[128,16,128]{2,1,0:T(8,128)(2,1)} %bitcast.7), calls=%async_computation | async-start | bytes 1048576 | tf_op jit(solution)/shard_map/all_to_all | solution.py:288
  26.6 27.3 %all-to-all-start.1 = ((bf16[128,48,128]{2,1,0:T(8,128)(2,1)}), bf16[128,48,128]{2,1,0:T(8,128)(2,1)S(1)}, u32[]{:S(2)}, u32[]{:S(2)}) async-start(bf16[128,48,128]{2,1,0:T(8,128)(2,1)} %shuffle.1), calls=%async_computation.1 | async-start | bytes 3145728 | tf_op jit(solution)/shard_map/all_to_all | solution.py:293
